TPU v7x, 32 devices: a whole 2x2x4 slice. The times are simulated.
32 devices in a mesh: seq: 8 (over y, x, core), tp: 4 (over z).
Axes of the slice: x: 2, y: 2, z: 4, core: 2. Of those that a mesh axis runs over, the one named last changes fastest.
Arguments:
- hidden_in: bfloat16 [4096, 2048], P('seq', 'tp'), may hold values from -60 to 60
- w_query: bfloat16 [2048, 2048], P(None, 'tp'), may hold values from -0.125 to 0.125
- w_key: bfloat16 [2048, 2048], P(None, 'tp'), may hold values from -0.125 to 0.125
- w_value: bfloat16 [2048, 2048], P(None, 'tp'), may hold values from -0.8984375 to 0.8984375
- w_pos: bfloat16 [2048, 2048], P(None, 'tp'), may hold values from -0.125 to 0.125
- w_out: bfloat16 [2048, 2048], P('tp'), may hold values from -0.125 to 0.125
- bias_content: float32 [16, 128], P('tp'), may hold values from -4 to 4
- bias_pos: float32 [16, 128], P('tp'), may hold values from -4 to 4
- norm_gain: float32 [2048], P('tp'), may hold values from 0.1 to 1.9
- norm_bias: float32 [2048], P('tp'), may hold values from -3 to 3
Outputs:
- hidden_out: bfloat16 [4096, 2048], P('seq', 'tp')
All inputs are finite; a program needn't handle non-finite values.
Results may differ from a plain program's by a relative error of at most 0.014.
The roundings to bfloat16 on the way count: a program that leaves them out, or rounds other values in their place, can miss the bound.
Values may be sent and summed in bfloat16 or wider, within the bound.
A program may use at most 128 MiB of HBM per device.

v0:
```python
import jax
import jax.numpy as jnp
from jax import lax
from jax.sharding import PartitionSpec as P


def shifted(block, axis, distance):
    devices = range(lax.axis_size(axis))
    route = [(i - distance, i) for i in devices if i - distance in devices]
    return lax.ppermute(block, axis, route)


def relative_table(span, width):
    half = width // 2
    freq = jnp.exp(-jnp.log(10000.0) * jnp.arange(half).astype(jnp.float32) / half)
    distance = (span - 1 - jnp.arange(span)).astype(jnp.float32)
    angle = distance[:, None] * freq[None, :]
    return jnp.concatenate([jnp.sin(angle), jnp.cos(angle)], 1).astype(jnp.bfloat16)


def shift_rows(table, seg, span):
    heads = table.shape[0]
    padded = jnp.pad(table, ((0, 0), (0, 0), (0, 1)))
    flat = padded.reshape(heads, seg * (span + 1))
    return flat[:, seg - 1 : seg - 1 + seg * span].reshape(heads, seg, span)


def shards(
    hidden_in, w_query, w_key, w_value, w_pos, w_out, bias_content, bias_pos, norm_gain, norm_bias
):
    seg = hidden_in.shape[0]
    heads = bias_content.shape[0]
    head_dim = bias_content.shape[1]
    width = heads * head_dim
    model_width = w_query.shape[0]
    span = 3 * seg
    memory = 2 * seg
    place = lax.axis_index("seq")
    own = lax.all_gather(hidden_in, "tp", axis=1, tiled=True)
    query = jnp.dot(own, w_query, preferred_element_type=jnp.float32).astype(jnp.bfloat16)
    own_keys = jnp.dot(own, w_key, preferred_element_type=jnp.float32).astype(jnp.bfloat16)
    own_values = jnp.dot(own, w_value, preferred_element_type=jnp.float32).astype(jnp.bfloat16)
    key_parts = []
    value_parts = []
    for distance in (2, 1):
        earlier_keys, earlier_values = shifted((own_keys, own_values), "seq", distance)
        key_parts.append(earlier_keys)
        value_parts.append(earlier_values)
    keys = jnp.concatenate(key_parts + [own_keys], 0)
    values = jnp.concatenate(value_parts + [own_values], 0)
    rel = jnp.dot(
        relative_table(span, model_width), w_pos, preferred_element_type=jnp.float32
    ).astype(jnp.bfloat16)
    rel = rel.reshape(span, heads, head_dim)
    keys = keys.reshape(span, heads, head_dim)
    values = values.reshape(span, heads, head_dim)
    q_rows = query.astype(jnp.float32).reshape(seg, heads, head_dim)
    content_q = (q_rows + bias_content[None]).astype(jnp.bfloat16)
    pos_q = (q_rows + bias_pos[None]).astype(jnp.bfloat16)
    content = jnp.einsum("ihd,jhd->hij", content_q, keys, preferred_element_type=jnp.float32)
    position = jnp.einsum("ihd,ehd->hie", pos_q, rel, preferred_element_type=jnp.float32)
    position = shift_rows(position, seg, span)
    score = (content + position) * (1.0 / jnp.sqrt(jnp.float32(head_dim)))
    row = jnp.arange(seg)[:, None]
    col = jnp.arange(span)[None, :]
    allowed = (col <= row + memory) & (place * seg - memory + col >= 0)
    score = jnp.where(allowed[None], score, jnp.float32(-1e30))
    probs = jax.nn.softmax(score, axis=-1).astype(jnp.bfloat16)
    attended = jnp.einsum("hij,jhd->ihd", probs, values, preferred_element_type=jnp.float32)
    attended = attended.astype(jnp.bfloat16).reshape(seg, width)
    partial_out = jnp.dot(attended, w_out, preferred_element_type=jnp.float32)
    branch = lax.psum_scatter(
        partial_out.astype(jnp.bfloat16), "tp", scatter_dimension=1, tiled=True
    ).astype(jnp.float32)
    summed = hidden_in.astype(jnp.float32) + branch
    total = lax.psum(jnp.sum(summed, axis=1), "tp")
    center = total / model_width
    centred = summed - center[:, None]
    spread = lax.psum(jnp.sum(centred * centred, axis=1), "tp") / model_width
    normed = centred / jnp.sqrt(spread[:, None] + 1e-05)
    return (normed * norm_gain[None] + norm_bias[None]).astype(jnp.bfloat16)


def solution(mesh):
    in_specs = (
        P("seq", "tp"),
        P(None, "tp"),
        P(None, "tp"),
        P(None, "tp"),
        P(None, "tp"),
        P("tp", None),
        P("tp", None),
        P("tp", None),
        P("tp"),
        P("tp"),
    )
    out_specs = P("seq", "tp")
    return jax.shard_map(shards, mesh=mesh, in_specs=in_specs, out_specs=out_specs, check_vma=False)
```

profile of v0, /device:TPU:0, one launch (start us, length us, event | category | flops | bytes accessed | tf_op | source)
XLA Modules:
  0.0 256.7 jit_solution(2363888968351827985)
XLA Ops:
  6.5 0.0 copy-start
  6.5 0.0 all-gather.2.cloned.1.call-start
  6.5 0.7 all-gather.2.cloned.1.call-update
  7.3 0.0 reduce-scatter.2.cloned.1.call-start
  7.4 0.6 fusion.10
  7.9 0.0 copy-start.7
  8.0 23.2 %fusion.3 = (bf16[1536,1024]{1,0:T(8,128)(2,1)S(1)}, bf16[1536,1024]{1,0:T(8,128)(2,1)S(1)}) fusion(f32[1024]{0:T(1024)S(1)} %multiply_exponential_fusion, f32[1536]{0:T(1024)S(1)} %subtract_convert_fusion), kind=kLoop, calls=%fused_computation.8 | loop fusion | flops 4718592 | bytes 6301696 | tf_op jit(solution)/shard_map/convert.1
  31.2 0.0 copy-done.7
  31.2 4.8 %fusion.11 = bf16[1536,512]{0,1:T(8,128)(2,1)} fusion(bf16[2048,512]{1,0:T(8,128)(2,1)S(1)} %copy-done.7, bf16[1536,1024]{1,0:T(8,128)(2,1)S(1)} %get-tuple-element.6, bf16[1536,1024]{1,0:T(8,128)(2,1)S(1)} %get-tuple-element.5), kind=kOutput, calls=%fused_computation.17 | convolution fusion | flops 3234594816 | bytes 9961472 | tf_op jit(solution)/shard_map/dot_general | solution.py:51
  36.1 21.3 %all-gather.2.cloned.1.call-done = bf16[512,2048]{1,0:T(8,128)(2,1)} async-done(((bf16[512,512]{1,0:T(8,128)(2,1)}), bf16[512,2048]{1,0:T(8,128)(2,1)}) %all-gather.2.cloned.1.call-update) | async-done | bytes 2097168 | tf_op jit(solution)/shard_map/all_gather | solution.py:39
  57.3 0.0 copy-start.8
  57.3 0.0 copy-start.10
  57.3 3.6 %convolution_convert_fusion.1 = bf16[512,512]{1,0:T(8,128)(2,1)S(1)} fusion(bf16[512,2048]{1,0:T(8,128)(2,1)} %all-gather.2.cloned.1.call-done, bf16[2048,512]{1,0:T(8,128)(2,1)} %param.12), kind=kOutput, calls=%fused_computation.23 | convolution fusion | flops 1074003968 | bytes 4718592 | tf_op jit(solution)/shard_map/dot_general | solution.py:41
  61.0 0.0 copy-start.9
  61.0 4.3 %collective-permute-start.2 = (bf16[512,512]{1,0:T(8,128)(2,1)S(1)}, bf16[512,512]{1,0:T(8,128)(2,1)}, u32[]{:S(2)}, u32[]{:S(2)}) collective-permute-start(bf16[512,512]{1,0:T(8,128)(2,1)S(1)} %convolution_convert_fusion.1), channel_id=1, source_target_pairs={{0,8},{4,12},{8,16},{12,20},{16,24},{20,28},{1,9},{5,13},{9,17},{1... | collective-permute-start | bytes 1572872 | tf_op jit(solution)/shard_map/ppermute | solution.py:10
  65.3 2.1 collective-permute-start.3
  67.4 0.0 copy-done.8
  67.4 0.0 copy-done.10
  67.4 2.0 convolution_convert_fusion.3
  69.4 0.0 copy-start.3
  69.4 3.3 %collective-permute-start = (bf16[512,512]{1,0:T(8,128)(2,1)}, bf16[512,512]{1,0:T(8,128)(2,1)}, u32[]{:S(2)}, u32[]{:S(2)}) collective-permute-start(bf16[512,512]{1,0:T(8,128)(2,1)} %convolution_convert_fusion.3), channel_id=1, source_target_pairs={{0,8},{4,12},{8,16},{12,20},{16,24},{20,28},{1,9},{5,13},{9,17},{1... | collective-permute-start | bytes 1572872 | tf_op jit(solution)/shard_map/ppermute | solution.py:10
  72.8 4.0 %collective-permute-start.1 = (bf16[512,512]{1,0:T(8,128)(2,1)}, bf16[512,512]{1,0:T(8,128)(2,1)}, u32[]{:S(2)}, u32[]{:S(2)}) collective-permute-start(bf16[512,512]{1,0:T(8,128)(2,1)} %convolution_convert_fusion.3), channel_id=1, source_target_pairs={{0,4},{4,8},{8,12},{12,16},{16,20},{20,24},{24,28},{1,5},{5,9},{9,... | collective-permute-start | bytes 1572872 | tf_op jit(solution)/shard_map/ppermute | solution.py:10
  76.8 0.0 copy-done.9
  76.8 2.1 convolution_convert_fusion.2
  78.9 2.2 copy.16
  81.1 0.0 copy-done.3
  81.1 8.1 %fusion.19 = f32[4,512,1536]{2,1,0:T(8,128)} fusion(bf16[1536,4,128]{0,2,1:T(8,128)(2,1)} %bitcast.35, f32[512,4,128]{2,0,1:T(8,128)} %copy.16, f32[4,128]{1,0:T(4,128)S(1)} %copy-done.3), kind=kOutput, calls=%fused_computation.34 | convolution fusion | flops 805830656 | bytes 15206400 | tf_op jit(solution)/shard_map/ihd,ehd->hie/dot_general | solution.py:61
  89.2 10.7 %pad.4 = f32[4,512,1537]{2,1,0:T(8,128)} pad(f32[4,512,1536]{2,1,0:T(8,128)} %fusion.19, f32[]{:T(128)} %constant.13.clone.1), padding=0_0x0_0x0_1 | pad | bytes 25174020 | tf_op jit(solution)/shard_map/jit(_pad)/pad | solution.py:23
  99.9 20.2 %reshape.101 = f32[3147776]{0:T(1024)} reshape(f32[4,512,1537]{2,1,0:T(8,128)} %pad.4) | data formatting | bytes 25182208
  120.1 15.0 %reshape.96 = f32[4,786944]{1,0:T(4,128)} reshape(f32[3147776]{0:T(1024)} %reshape.101) | data formatting | bytes 25182208 | tf_op jit(solution)/shard_map/reshape | solution.py:24
  135.1 0.0 copy-start.1
  135.1 0.0 copy-start.4
  135.1 9.7 %slice.4 = f32[4,786432]{1,0:T(4,128)S(1)} slice(f32[4,786944]{1,0:T(4,128)} %reshape.96), slice={[0:4], [511:786943]} | slice | bytes 25165824 | tf_op jit(solution)/shard_map/slice | solution.py:25
  144.7 0.0 collective-permute-done.2
  144.8 0.0 collective-permute-done.3
  144.8 0.0 copy-done.1
  144.8 0.0 copy-done.4
  144.8 11.5 %fusion.2 = f32[4,512,1536]{2,1,0:T(8,128)} fusion(f32[1,4,512,1536]{3,1,2,0:T(4,128)S(1)} %bitcast.34, pred[512,1536]{1,0:T(8,128)(4,1)S(1)} %fusion.10, f32[512,4,128]{2,0,1:T(8,128)S(1)} %copy-done.1, f32[4,128]{1,0:T(4,128)S(1)} %copy-done.4, bf16[512,512]{1,0:T(8,128)(2,1)S(1)} %convolution_convert_fusion.1, ...), kind=kOutput, calls=%fused_computation.3 | convolution fusion | flops 819986432 | bytes 28575744 | tf_op jit(solution)/shard_map/ihd,jhd->hij/dot_general | solution.py:60
  156.3 10.4 %fusion.24 = f32[4,512]{1,0:T(4,128)S(1)} fusion(f32[4,512,1536]{2,1,0:T(8,128)} %fusion.2), kind=kOutput, calls=%fused_computation.45 | output fusion | flops 6292991 | bytes 12591104 | tf_op jit(solution)/shard_map/sub | solution.py:68
  166.8 0.0 collective-permute-done
  166.8 0.0 collective-permute-done.1
  166.8 2.6 %pad_maximum_fusion = bf16[1536,512]{1,0:T(8,128)(2,1)} fusion(bf16[512,512]{1,0:T(8,128)(2,1)} %convolution_convert_fusion.3, bf16[512,512]{1,0:T(8,128)(2,1)} %collective-permute-done.1, bf16[512,512]{1,0:T(8,128)(2,1)} %collective-permute-done), kind=kLoop, calls=%fused_computation.21 | loop fusion | flops 4718592 | bytes 3145728 | tf_op jit(solution)/shard_map/concatenate | solution.py:50
  169.4 2.6 %copy.22 = bf16[1536,512]{0,1:T(8,128)(2,1)} copy(bf16[1536,512]{1,0:T(8,128)(2,1)} %pad_maximum_fusion) | data formatting | bytes 3145728 | tf_op jit(solution)/shard_map/reshape | solution.py:56
  172.0 10.9 %fusion.16 = bf16[4,128,512]{2,1,0:T(8,128)(2,1)S(1)} fusion(bf16[1536,4,128]{0,2,1:T(8,128)(2,1)} %bitcast.36, f32[4,512]{1,0:T(4,128)S(1)} %fusion.24, f32[4,512,1536]{2,1,0:T(8,128)} %fusion.2), kind=kOutput, calls=%fused_computation.26 | convolution fusion | flops 815009280 | bytes 14688256 | tf_op jit(solution)/shard_map/hij,jhd->ihd/dot_general | solution.py:69
  182.9 0.0 copy-done
  182.9 0.0 copy-start.2
  182.9 2.6 %convolution_convert_fusion = bf16[512,2048]{1,0:T(8,128)(2,1)} fusion(bf16[512,512]{0,1:T(8,128)(2,1)S(1)} %bitcast.38, bf16[512,2048]{1,0:T(8,128)(2,1)S(1)} %copy-done), kind=kOutput, calls=%fused_computation.18 | convolution fusion | flops 1074790400 | bytes 4718592 | tf_op jit(solution)/shard_map/dot_general | solution.py:71
  185.6 0.0 copy-start.5
  185.6 0.0 copy-start.6
  185.6 0.0 reduce-scatter.2.cloned.1.call-update
  185.6 40.8 %reduce-scatter.2.cloned.1.call-done = bf16[512,512]{1,0:T(8,128)(2,1)} async-done(((bf16[512,2048]{1,0:T(8,128)(2,1)}), bf16[512,512]{1,0:T(8,128)(2,1)}) %reduce-scatter.2.cloned.1.call-update) | async-done | bytes 524304 | tf_op jit(solution)/shard_map/reduce_scatter | solution.py:72
  226.4 0.0 copy-done.2
  226.4 1.3 fusion.18
  227.6 10.2 %psum.14 = f32[512]{0:T(512)S(1)} all-reduce(f32[512]{0:T(512)S(1)} %fusion.18), channel_id=1, replica_groups=mesh['seq'=8,'tp'=4] {'tp'}, use_global_device_ids=true, to_apply=%region_4.5 | all-reduce | flops 512 | bytes 4096 | tf_op jit(solution)/shard_map/psum | solution.py:76
  237.8 1.3 multiply_reduce_fusion
  239.1 8.6 %psum.15 = f32[512]{0:T(512)S(1)} all-reduce(f32[512]{0:T(512)S(1)} %multiply_reduce_fusion), channel_id=1, replica_groups=mesh['seq'=8,'tp'=4] {'tp'}, use_global_device_ids=true, to_apply=%region_6.7 | all-reduce | flops 512 | bytes 4096 | tf_op jit(solution)/shard_map/psum | solution.py:79
  247.7 0.0 copy-done.5
  247.7 0.0 copy-done.6
  247.7 2.1 add_convert_fusion
  (6 shorter events, 0.0 us)
Async XLA Ops:
  6.5 176.4 %copy-start = (bf16[512,2048]{1,0:T(8,128)(2,1)S(1)}, bf16[512,2048]{1,0:T(8,128)(2,1)}, u32[]{:S(2)}) copy-start(bf16[512,2048]{1,0:T(8,128)(2,1)} %param.15) | copy-start | bytes 6291460
  6.5 50.8 %all-gather.2.cloned.1.call-start = ((), (), s32[]{:S(2)}) async-start(), calls=%async_computation.1 | async-start | bytes 2621440 | tf_op jit(solution)/shard_map/all_gather | solution.py:39
  7.3 219.1 %reduce-scatter.2.cloned.1.call-start = ((), (), s32[]{:S(2)}) async-start(), calls=%async_computation.2 | async-start | bytes 2621440 | tf_op jit(solution)/shard_map/reduce_scatter | solution.py:72
  7.9 23.3 %copy-start.7 = (bf16[2048,512]{1,0:T(8,128)(2,1)S(1)}, bf16[2048,512]{1,0:T(8,128)(2,1)}, u32[]{:S(2)}) copy-start(bf16[2048,512]{1,0:T(8,128)(2,1)} %param.14) | copy-start | bytes 6291460
  57.3 10.1 %copy-start.8 = (bf16[2048,512]{1,0:T(8,128)(2,1)S(1)}, bf16[2048,512]{1,0:T(8,128)(2,1)}, u32[]{:S(2)}) copy-start(bf16[2048,512]{1,0:T(8,128)(2,1)} %param.13) | copy-start | bytes 6291460
  57.3 10.1 %copy-start.10 = (bf16[512,2048]{1,0:T(8,128)(2,1)S(1)}, bf16[512,2048]{1,0:T(8,128)(2,1)}, u32[]{:S(2)}) copy-start(bf16[512,2048]{1,0:T(8,128)(2,1)} %all-gather.2.cloned.1.call-done) | copy-start | bytes 6291460
  61.0 15.8 %copy-start.9 = (bf16[2048,512]{1,0:T(8,128)(2,1)S(1)}, bf16[2048,512]{1,0:T(8,128)(2,1)}, u32[]{:S(2)}) copy-start(bf16[2048,512]{1,0:T(8,128)(2,1)} %param.11) | copy-start | bytes 6291460
  61.0 83.8 %collective-permute-start.2 = (bf16[512,512]{1,0:T(8,128)(2,1)S(1)}, bf16[512,512]{1,0:T(8,128)(2,1)}, u32[]{:S(2)}, u32[]{:S(2)}) collective-permute-start(bf16[512,512]{1,0:T(8,128)(2,1)S(1)} %convolution_convert_fusion.1), channel_id=1, source_target_pairs={{0,8},{4,12},{8,16},{12,20},{16,24},{20,28},{1,9},{5,13},{9,17},{1... | collective-permute-start | bytes 1572872 | tf_op jit(solution)/shard_map/ppermute | solution.py:10
  65.3 79.5 %collective-permute-start.3 = (bf16[512,512]{1,0:T(8,128)(2,1)S(1)}, bf16[512,512]{1,0:T(8,128)(2,1)}, u32[]{:S(2)}, u32[]{:S(2)}) collective-permute-start(bf16[512,512]{1,0:T(8,128)(2,1)S(1)} %convolution_convert_fusion.1), channel_id=1, source_target_pairs={{0,4},{4,8},{8,12},{12,16},{16,20},{20,24},{24,28},{1,5},{5,9},{9,... | collective-permute-start | bytes 1572872 | tf_op jit(solution)/shard_map/ppermute | solution.py:10
  69.4 11.7 %copy-start.3 = (f32[4,128]{1,0:T(4,128)S(1)}, f32[4,128]{1,0:T(4,128)}, u32[]{:S(2)}) copy-start(f32[4,128]{1,0:T(4,128)} %param.17) | copy-start | bytes 6148
  69.4 97.3 %collective-permute-start = (bf16[512,512]{1,0:T(8,128)(2,1)}, bf16[512,512]{1,0:T(8,128)(2,1)}, u32[]{:S(2)}, u32[]{:S(2)}) collective-permute-start(bf16[512,512]{1,0:T(8,128)(2,1)} %convolution_convert_fusion.3), channel_id=1, source_target_pairs={{0,8},{4,12},{8,16},{12,20},{16,24},{20,28},{1,9},{5,13},{9,17},{1... | collective-permute-start | bytes 1572872 | tf_op jit(solution)/shard_map/ppermute | solution.py:10
  72.8 94.0 %collective-permute-start.1 = (bf16[512,512]{1,0:T(8,128)(2,1)}, bf16[512,512]{1,0:T(8,128)(2,1)}, u32[]{:S(2)}, u32[]{:S(2)}) collective-permute-start(bf16[512,512]{1,0:T(8,128)(2,1)} %convolution_convert_fusion.3), channel_id=1, source_target_pairs={{0,4},{4,8},{8,12},{12,16},{16,20},{20,24},{24,28},{1,5},{5,9},{9,... | collective-permute-start | bytes 1572872 | tf_op jit(solution)/shard_map/ppermute | solution.py:10
  135.1 9.7 %copy-start.1 = (f32[512,4,128]{2,0,1:T(8,128)S(1)}, f32[512,4,128]{2,0,1:T(8,128)}, u32[]{:S(2)}) copy-start(f32[512,4,128]{2,0,1:T(8,128)} %copy.16) | copy-start | bytes 3145732
  135.1 9.7 %copy-start.4 = (f32[4,128]{1,0:T(4,128)S(1)}, f32[4,128]{1,0:T(4,128)}, u32[]{:S(2)}) copy-start(f32[4,128]{1,0:T(4,128)} %param.16) | copy-start | bytes 6148
  182.9 43.4 %copy-start.2 = (bf16[512,512]{1,0:T(8,128)(2,1)S(1)}, bf16[512,512]{1,0:T(8,128)(2,1)}, u32[]{:S(2)}) copy-start(bf16[512,512]{1,0:T(8,128)(2,1)} %param.10) | copy-start | bytes 1572868
  185.6 62.1 %copy-start.5 = (f32[512]{0:T(512)S(1)}, f32[512]{0:T(512)}, u32[]{:S(2)}) copy-start(f32[512]{0:T(512)} %param.19) | copy-start | bytes 6148
  185.6 62.1 %copy-start.6 = (f32[512]{0:T(512)S(1)}, f32[512]{0:T(512)}, u32[]{:S(2)}) copy-start(f32[512]{0:T(512)} %param.18) | copy-start | bytes 6148
Sparse Core Ops, SparseCore 0:
  8.9 48.3 all-gather.1
  185.7 40.5 reduce-scatter.1
where the time goes:
time: 257 us
  waiting for transfers between devices  62.8 us (24%)
  local copies, waits for them, and re-layouts  60.4 us (24%)
  matrix products  45.7 us (18%)
  other arithmetic  41.6 us (16%)
  blocking collectives  18.7 us (7%)
  starting transfers between devices  13.8 us (5%)
  between operations  13.6 us (5%)
    reduce_scatter x1, waiting for transfers between devices, shards(): lax.psum_scatter(partial_out.astype(jnp.bfloat16), 'tp', scatter_dimensio...  40.8 us
    another operation x1, other arithmetic  23.2 us
    all_gather x1, waiting for transfers between devices, shards(): own = lax.all_gather(hidden_in, 'tp', axis=1, tiled=True)  21.3 us
    unnamed x23, local copies, waits for them, and re-layouts  20.3 us
    reshape x1, local copies, waits for them, and re-layouts, shift_rows(): flat = padded.reshape(heads, seg * (span + 1))  15 us
    ppermute x4, starting transfers between devices, shifted(): return lax.ppermute(block, axis, route)  13.8 us
    dot_general x1, matrix products, shards(): jnp.einsum('ihd,jhd->hij', content_q, keys, preferred_element_type=jnp.fl...  11.5 us
    dot_general x1, matrix products, shards(): jnp.einsum('hij,jhd->ihd', probs, values, preferred_element_type=jnp.floa...  10.9 us
  transfers between devices with their start and end apart: 6, of which 2 were waited for; matrix products, arithmetic and copies ran while one was open for 47% of the time, Pallas kernels for 0%

commit v1 on v0

v1 whole, which is shorter than its diff:
```python
import functools

import jax
import jax.numpy as jnp
import numpy as np
from jax import lax
from jax.experimental import pallas as pl
from jax.experimental.pallas import tpu as pltpu
from jax.sharding import PartitionSpec as P

F32 = jnp.float32
BF16 = jnp.bfloat16
ROWS = 128


def angle_tables(span, width):
    half = width // 2
    freq = np.exp(-np.log(10000.0) * np.arange(half) / half)
    fine = (ROWS - 1 - np.arange(ROWS))[:, None] * freq[None]
    blocks = span // ROWS
    coarse = (ROWS * (blocks - 1 - np.arange(blocks)))[:, None] * freq[None]
    pack = lambda a: np.concatenate([np.sin(a), np.cos(a)], 1).astype(np.float32)
    return pack(fine), pack(coarse)


def kernel(
    n_seq,
    n_tp,
    hidden,
    wq_hbm,
    wk_hbm,
    wv_hbm,
    wpos_hbm,
    wout_hbm,
    fine_hbm,
    coarse,
    bias_c,
    bias_p,
    gain,
    shift,
    out,
    w_all,
    w_pos,
    w_out,
    fine,
    full,
    k_t,
    val,
    rel_t,
    emb,
    cq,
    pq,
    att,
    sum_own,
    part,
    got,
    stat,
    stat_got,
    local_sem,
    ag_send,
    ag_recv,
    kv_send,
    kv_recv,
    rs_send,
    rs_recv,
    st_send,
    st_recv,
):
    seg, feat = hidden.shape
    heads, head_dim = bias_c.shape
    width = heads * head_dim
    model = n_tp * feat
    span = 3 * seg
    memory = 2 * seg
    chunks = seg // ROWS
    me = lax.axis_index("tp")
    place = lax.axis_index("seq")
    right = lax.rem(me + 1, n_tp)
    left = lax.rem(me + n_tp - 1, n_tp)
    opp = lax.rem(me + 2, n_tp)
    following = lax.rem(place + 1, n_seq)
    before = lax.rem(place + n_seq - 1, n_seq)

    loads = []
    for i, (src, dst) in enumerate(
        (
            (fine_hbm, fine),
            (wpos_hbm, w_pos),
            (wq_hbm, w_all.at[:, 0:width]),
            (wk_hbm, w_all.at[:, width : 2 * width]),
            (wv_hbm, w_all.at[:, 2 * width : 3 * width]),
            (wout_hbm, w_out),
        )
    ):
        load = pltpu.make_async_copy(src, dst, local_sem.at[i])
        load.start()
        loads.append(load)

    barrier = pltpu.get_barrier_semaphore()
    for peer in ({"tp": right}, {"tp": left}, {"tp": opp}, {"seq": following}, {"seq": before}):
        pl.semaphore_signal(barrier, inc=1, device_id=peer, device_id_type=pl.DeviceIdType.MESH)
    pl.semaphore_wait(barrier, 5)

    sent = []

    def send(src, dst, send_sem, recv_sem, peer):
        copy = pltpu.make_async_remote_copy(
            src_ref=src,
            dst_ref=dst,
            send_sem=send_sem,
            recv_sem=recv_sem,
            device_id=peer,
            device_id_type=pl.DeviceIdType.MESH,
        )
        copy.start()
        sent.append(copy)
        return copy

    def rows(c):
        return slice(c * ROWS, (c + 1) * ROWS)

    def cols_of(owner):
        return pl.ds(pl.multiple_of(owner * feat, feat), feat)

    def share(c):
        dst = full.at[rows(c), cols_of(me)]
        src = hidden.at[rows(c), :]
        a = send(src, dst, ag_send.at[0, c], ag_recv.at[0, c], {"tp": right})
        b = send(src, dst, ag_send.at[1, c], ag_recv.at[1, c], {"tp": left})
        return a, b

    def relay(c, pair):
        pair[0].wait_recv()
        pair[1].wait_recv()
        owner, peer = (left, right) if c % 2 == 0 else (right, left)
        block = full.at[rows(c), cols_of(owner)]
        return send(block, block, ag_send.at[2, c], ag_recv.at[2, c], {"tp": peer})

    half = model // 2

    def rel_block(b):
        for k in range(2):
            at = pl.ds(2 * b + k, 1)
            c_sin, c_cos = coarse[at, :half], coarse[at, half:]
            f_sin, f_cos = fine[:, :half], fine[:, half:]
            emb[rows(k), :half] = (c_sin * f_cos + c_cos * f_sin).astype(BF16)
            emb[rows(k), half:] = (c_cos * f_cos - c_sin * f_sin).astype(BF16)
        block = jnp.dot(emb[...], w_pos[...], preferred_element_type=F32)
        at = pl.ds(pl.multiple_of(b * 2 * ROWS, 2 * ROWS), 2 * ROWS)
        rel_t[:, at] = block.T.astype(BF16)

    blocks = span // (2 * ROWS)
    rel_cuts = [blocks * i // 3 for i in range(4)]

    def rel_some(i):
        def one(b, carry):
            rel_block(b)
            return carry

        lax.fori_loop(rel_cuts[i], rel_cuts[i + 1], one, 0)

    def project(c):
        x = full[rows(c), :]
        q = jnp.dot(x, w_all[:, :width], preferred_element_type=F32).astype(BF16).astype(F32)
        k = jnp.dot(x, w_all[:, width : 2 * width], preferred_element_type=F32)
        v = jnp.dot(x, w_all[:, 2 * width :], preferred_element_type=F32)
        lo = memory + c * ROWS
        k_t[:, lo : lo + ROWS] = k.T.astype(BF16)
        val[lo : lo + ROWS, :] = v.astype(BF16)
        for h in range(heads):
            at = slice(h * head_dim, (h + 1) * head_dim)
            cq[rows(c), at] = (q[:, at] + bias_c[h : h + 1, :]).astype(BF16)
            pq[rows(c), at] = (q[:, at] + bias_p[h : h + 1, :]).astype(BF16)

    def pass_on(hop, c):
        lo = (2 - hop) * seg + c * ROWS
        to = lo - seg
        peer = {"seq": following}
        a = send(
            k_t.at[:, lo : lo + ROWS],
            k_t.at[:, to : to + ROWS],
            kv_send.at[hop, 0, c],
            kv_recv.at[hop, 0, c],
            peer,
        )
        b = send(
            val.at[lo : lo + ROWS, :],
            val.at[to : to + ROWS, :],
            kv_send.at[hop, 1, c],
            kv_recv.at[hop, 1, c],
            peer,
        )
        return a, b

    pairs = [share(c) for c in range(2)]
    full[:, cols_of(me)] = hidden[...]
    loads[0].wait()
    loads[1].wait()
    relays, hops = [], [[], []]
    for c in range(chunks):
        if c < 3:
            rel_some(c)
        relays.append(relay(c, pairs[c]))
        if c + 2 < chunks:
            pairs.append(share(c + 2))
        if c == 1:
            for load in loads[2:5]:
                load.wait()
        if c >= 1:
            relays[c - 1].wait_recv()
            project(c - 1)
            hops[0].append(pass_on(0, c - 1))
    relays[-1].wait_recv()
    project(chunks - 1)
    hops[0].append(pass_on(0, chunks - 1))
    for c in range(chunks):
        for copy in hops[0][c]:
            copy.wait_recv()
        hops[1].append(pass_on(1, c))
    loads[5].wait()
    for c in range(chunks):
        for copy in hops[1][c]:
            copy.wait_recv()

    factor = np.float32(np.log2(np.e) / np.sqrt(head_dim))
    edge = jnp.maximum(memory - place * seg, 0)

    def attend(r, h, low):
        length = memory + (r + 1) * ROWS
        at = pl.ds(pl.multiple_of(h * head_dim, head_dim), head_dim)
        content = jnp.dot(cq[rows(r), at], k_t[at, :length], preferred_element_type=F32)
        position = jnp.dot(pq[rows(r), at], rel_t[at, span - length :], preferred_element_type=F32)
        position = pltpu.roll(position, length - (ROWS - 1), 1, stride=1, stride_axis=0)
        score = content + position + low
        last = score[:, length - ROWS :]
        i = lax.broadcasted_iota(jnp.int32, (ROWS, ROWS), 0)
        j = lax.broadcasted_iota(jnp.int32, (ROWS, ROWS), 1)
        last = jnp.where(j <= i, last, -1e30)
        score = jnp.concatenate([score[:, : length - ROWS], last], 1)
        top = jnp.max(score, axis=1, keepdims=True)
        e = jnp.exp2((score - top) * factor)
        probs = (e * (1.0 / jnp.sum(e, axis=1, keepdims=True))).astype(BF16)
        res = jnp.dot(probs, val[:length, at], preferred_element_type=F32)
        att[:, at] = res.astype(BF16)

    def product(owner):
        return jnp.dot(att[...], w_out[:, cols_of(owner)], preferred_element_type=F32).astype(BF16)

    scatter = [[None] * chunks for _ in range(3)]

    def ways(r):
        return (right, left) if r % 2 == 0 else (left, right)

    def scatter_first(r):
        ahead, back = ways(r)
        part[0, rows(r), :] = product(opp)
        scatter[0][r] = send(
            part.at[0, rows(r), :],
            got.at[0, rows(r), :],
            rs_send.at[0, r],
            rs_recv.at[0, r],
            {"tp": ahead},
        )
        part[1, rows(r), :] = product(back)
        scatter[1][r] = send(
            part.at[1, rows(r), :],
            got.at[1, rows(r), :],
            rs_send.at[1, r],
            rs_recv.at[1, r],
            {"tp": back},
        )
        part[2, rows(r), :] = product(ahead)
        sum_own[rows(r), :] = hidden[rows(r), :].astype(F32) + product(me).astype(F32)

    def scatter_second(r):
        ahead, _ = ways(r)
        scatter[0][r].wait_recv()
        both = part[2, rows(r), :].astype(F32) + got[0, rows(r), :].astype(F32)
        part[2, rows(r), :] = both.astype(BF16)
        scatter[2][r] = send(
            part.at[2, rows(r), :],
            got.at[2, rows(r), :],
            rs_send.at[2, r],
            rs_recv.at[2, r],
            {"tp": ahead},
        )

    stats = [None] * chunks

    def moments(r):
        scatter[1][r].wait_recv()
        scatter[2][r].wait_recv()
        y = sum_own[rows(r), :] + got[1, rows(r), :].astype(F32) + got[2, rows(r), :].astype(F32)
        sum_own[rows(r), :] = y
        total = jnp.sum(y, axis=1, keepdims=True)
        off = y - total * (1.0 / feat)
        square = jnp.sum(off * off, axis=1, keepdims=True)
        lane = lax.broadcasted_iota(jnp.int32, (ROWS, ROWS), 1)
        tile = jnp.where(lane == 0, total, square)
        stat[r] = tile.T[:8, :]
        stats[r] = [
            send(stat.at[r], stat_got.at[i, r], st_send.at[i, r], st_recv.at[i, r], {"tp": peer})
            for i, peer in enumerate((right, left, opp))
        ]

    def finish(r):
        for copy in stats[r]:
            copy.wait_recv()
        all_of = [stat[r]] + [stat_got[i, r] for i in range(3)]
        totals = [a[0:1, :] for a in all_of]
        squares = [a[1:2, :] for a in all_of]
        center = sum(totals[1:], totals[0]) * (1.0 / model)
        spread = sum(squares[1:], squares[0])
        for t in totals:
            gap = t * (1.0 / feat) - center
            spread = spread + feat * (gap * gap)
        inverse = 1.0 / jnp.sqrt(spread * (1.0 / model) + 1e-05)
        center = jnp.broadcast_to(center, (ROWS, ROWS)).T
        inverse = jnp.broadcast_to(inverse, (ROWS, ROWS)).T
        for p in range(feat // ROWS):
            at = slice(p * ROWS, (p + 1) * ROWS)
            y = (sum_own[rows(r), at] - center) * inverse
            out[rows(r), at] = (y * gain[:, at] + shift[:, at]).astype(BF16)

    for r in range(chunks):
        length = memory + (r + 1) * ROWS
        col = lax.broadcasted_iota(jnp.int32, (1, length), 1)
        low = jnp.where(col >= edge, 0.0, -1e30).astype(F32)

        def two(p, carry):
            attend(r, 2 * p, low)
            attend(r, 2 * p + 1, low)
            return carry

        lax.fori_loop(0, heads // 2, two, 0)
        scatter_first(r)
        if r >= 1:
            scatter_second(r - 1)
        if r >= 2:
            moments(r - 2)
    scatter_second(chunks - 1)
    moments(chunks - 2)
    moments(chunks - 1)
    for r in range(chunks):
        finish(r)
    for copy in sent:
        copy.wait_send()


def shards(n_seq, n_tp, hidden_in, wq, wk, wv, w_pos, w_out, bias_c, bias_p, gain, shift):
    seg, feat = hidden_in.shape
    heads, head_dim = bias_c.shape
    model, width = wq.shape
    span = 3 * seg
    chunks = seg // ROWS
    fine, coarse = angle_tables(span, model)
    any_spec = pl.BlockSpec(memory_space=pl.ANY)
    vmem = pl.BlockSpec(memory_space=pltpu.VMEM)
    dma = pltpu.SemaphoreType.DMA
    return pl.pallas_call(
        functools.partial(kernel, n_seq, n_tp),
        out_shape=jax.ShapeDtypeStruct((seg, feat), BF16),
        in_specs=[vmem] + [any_spec] * 6 + [vmem] * 5,
        out_specs=vmem,
        scratch_shapes=[
            pltpu.VMEM((model, 3 * width), BF16),
            pltpu.VMEM((model, width), BF16),
            pltpu.VMEM((width, model), BF16),
            pltpu.VMEM((ROWS, model), F32),
            pltpu.VMEM((seg, model), BF16),
            pltpu.VMEM((width, span), BF16),
            pltpu.VMEM((span, width), BF16),
            pltpu.VMEM((width, span), BF16),
            pltpu.VMEM((2 * ROWS, model), BF16),
            pltpu.VMEM((seg, width), BF16),
            pltpu.VMEM((seg, width), BF16),
            pltpu.VMEM((ROWS, width), BF16),
            pltpu.VMEM((seg, feat), F32),
            pltpu.VMEM((3, seg, feat), BF16),
            pltpu.VMEM((3, seg, feat), BF16),
            pltpu.VMEM((chunks, 8, ROWS), F32),
            pltpu.VMEM((3, chunks, 8, ROWS), F32),
            dma((6,)),
            dma((3, chunks)),
            dma((3, chunks)),
            dma((2, 2, chunks)),
            dma((2, 2, chunks)),
            dma((3, chunks)),
            dma((3, chunks)),
            dma((3, chunks)),
            dma((3, chunks)),
        ],
        compiler_params=pltpu.CompilerParams(
            collective_id=0, has_side_effects=True, vmem_limit_bytes=60 * 1024 * 1024
        ),
        name="layer",
    )(
        hidden_in,
        wq,
        wk,
        wv,
        w_pos,
        w_out,
        jnp.asarray(fine),
        jnp.asarray(coarse),
        bias_c,
        bias_p,
        gain.reshape(1, feat),
        shift.reshape(1, feat),
    )


def solution(mesh):
    in_specs = (
        P("seq", "tp"),
        P(None, "tp"),
        P(None, "tp"),
        P(None, "tp"),
        P(None, "tp"),
        P("tp", None),
        P("tp", None),
        P("tp", None),
        P("tp"),
        P("tp"),
    )
    return jax.shard_map(
        functools.partial(shards, mesh.shape["seq"], mesh.shape["tp"]),
        mesh=mesh,
        in_specs=in_specs,
        out_specs=P("seq", "tp"),
        check_vma=False,
    )
```

time: 257 us -> 101 us (0.39)
  Pallas kernels: 0 us -> 99 us
  waiting for transfers between devices: 62.8 us -> 0 us
  local copies, waits for them, and re-layouts: 60.4 us -> 1.87 us
  matrix products: 45.7 us -> 0 us
  other arithmetic: 41.6 us -> 0 us
  blocking collectives: 18.7 us -> 0 us
  starting transfers between devices: 13.8 us -> 0 us
  between operations: 13.6 us -> 0.01 us
    pallas_call x0 -> x1, Pallas kernels: none -> 99 us  [shards(): pl.pallas_call(functools.partial(kernel, n_seq, n_tp), out_shape=jax.Shap...]
    dot_general x8 -> x0, matrix products: 45.7 us -> none  [the longest x1 11.5 us: shards(): jnp.einsum('ihd,jhd->hij', content_q, keys, preferred_element_type=jnp.fl...]
    reduce_scatter x1 -> x0, waiting for transfers between devices: 40.8 us -> none  [shards(): lax.psum_scatter(partial_out.astype(jnp.bfloat16), 'tp', scatter_dimensio...]
    another operation x1 -> x0, other arithmetic: 23.2 us -> none
    all_gather x1 -> x0, waiting for transfers between devices: 21.3 us -> none  [shards(): own = lax.all_gather(hidden_in, 'tp', axis=1, tiled=True)]
    reshape x3 -> x0, local copies, waits for them, and re-layouts: 19.8 us -> none  [the longest x1 15 us: shift_rows(): flat = padded.reshape(heads, seg * (span + 1))]
    psum x2 -> x0, blocking collectives: 18.7 us -> none  [the longest x1 10.2 us: shards(): total = lax.psum(jnp.sum(summed, axis=1), 'tp')]
    unnamed x23 -> x1, local copies, waits for them, and re-layouts: 20.3 us -> 1.87 us
  transfers between devices with their start and end apart: 6 -> 0, of which waited for: 2 -> 0; matrix products, arithmetic and copies ran while one was open for 47% -> 0% of each run, Pallas kernels for 0% -> 0%
where the time goes in v1:
time: 101 us
  Pallas kernels  99 us (98%)
  local copies, waits for them, and re-layouts  1.87 us (2%)
    pallas_call x1, Pallas kernels, shards(): pl.pallas_call(functools.partial(kernel, n_seq, n_tp), out_shape=jax.Shap...  99 us

profile of v1, /device:TPU:0, one launch (start us, length us, event | category | flops | bytes accessed | tf_op | source)
XLA Modules:
  0.0 100.8 jit_solution(1428773310343068157)
XLA Ops:
  0.0 99.0 %layer.1 = bf16[512,512]{1,0:T(8,128)(2,1)} custom-call(bf16[512,512]{1,0:T(8,128)(2,1)} %hidden.1, bf16[2048,512]{1,0:T(8,128)(2,1)} %wq_hbm.1, bf16[2048,512]{1,0:T(8,128)(2,1)} %wk_hbm.1, bf16[2048,512]{1,0:T(8,128)(2,1)} %wv_hbm.1, bf16[2048,512]{1,0:T(8,128)(2,1)} %wpos_hbm.1, bf16[512,2048]{1,0:T(8,128)(2,1)} %wout_hbm.1, ...), custom_call_target="tpu_custom_call" | custom-call | tf_op jit(solution)/shard_map/layer/pallas_call | solution.py:360
  99.0 1.9 %copy.14 = bf16[512,512]{1,0:T(8,128)(2,1)} copy(bf16[512,512]{1,0:T(8,128)(2,1)} %layer.1) | data formatting | bytes 1048576

commit v2 on v1

--- a/solution.py
+++ b/solution.py
@@ -122,18 +122,24 @@
     def cols_of(owner):
         return pl.ds(pl.multiple_of(owner * feat, feat), feat)
 
-    def share(c):
-        dst = full.at[rows(c), cols_of(me)]
-        src = hidden.at[rows(c), :]
-        a = send(src, dst, ag_send.at[0, c], ag_recv.at[0, c], {"tp": right})
-        b = send(src, dst, ag_send.at[1, c], ag_recv.at[1, c], {"tp": left})
-        return a, b
-
-    def relay(c, pair):
-        pair[0].wait_recv()
-        pair[1].wait_recv()
-        owner, peer = (left, right) if c % 2 == 0 else (right, left)
-        block = full.at[rows(c), cols_of(owner)]
+    step = ROWS // 2
+
+    def piece(c):
+        return slice(c * step, (c + 1) * step)
+
+    def share(way, c):
+        peer = left if way else right
+        return send(
+            hidden.at[piece(c), :],
+            full.at[piece(c), cols_of(me)],
+            ag_send.at[way, c],
+            ag_recv.at[way, c],
+            {"tp": peer},
+        )
+
+    def relay(way, c):
+        owner, peer = (right, left) if way else (left, right)
+        block = full.at[piece(c), cols_of(owner)]
         return send(block, block, ag_send.at[2, c], ag_recv.at[2, c], {"tp": peer})
 
     half = model // 2
@@ -150,7 +156,7 @@
         rel_t[:, at] = block.T.astype(BF16)
 
     blocks = span // (2 * ROWS)
-    rel_cuts = [blocks * i // 3 for i in range(4)]
+    rel_cuts = [blocks * i // chunks for i in range(chunks + 1)]
 
     def rel_some(i):
         def one(b, carry):
@@ -192,31 +198,47 @@
         )
         return a, b
 
-    pairs = [share(c) for c in range(2)]
+    order = [[c + way if c % 2 == 0 else c - way for c in range(2 * chunks)] for way in range(2)]
+    shared, relays, hops = {}, {}, [[], []]
+
+    def share_next(first, last):
+        for at in range(first, min(last, 2 * chunks)):
+            for way in range(2):
+                shared[way, order[way][at]] = share(way, order[way][at])
+
+    def gathered(p):
+        shared[0, 2 * p + 1].wait_recv()
+        shared[1, 2 * p].wait_recv()
+        relays[2 * p].wait_recv()
+        relays[2 * p + 1].wait_recv()
+        project(p)
+        hops[0].append(pass_on(0, p))
+
+    def forward(p):
+        for copy in hops[0][p]:
+            copy.wait_recv()
+        hops[1].append(pass_on(1, p))
+
+    share_next(0, 3)
     full[:, cols_of(me)] = hidden[...]
     loads[0].wait()
     loads[1].wait()
-    relays, hops = [], [[], []]
-    for c in range(chunks):
-        if c < 3:
-            rel_some(c)
-        relays.append(relay(c, pairs[c]))
-        if c + 2 < chunks:
-            pairs.append(share(c + 2))
-        if c == 1:
+    for p in range(chunks):
+        for way in range(2):
+            shared[way, 2 * p + way].wait_recv()
+            relays[2 * p + way] = relay(way, 2 * p + way)
+        share_next(2 * p + 3, 2 * p + 5)
+        if p == 1:
             for load in loads[2:5]:
                 load.wait()
-        if c >= 1:
-            relays[c - 1].wait_recv()
-            project(c - 1)
-            hops[0].append(pass_on(0, c - 1))
-    relays[-1].wait_recv()
-    project(chunks - 1)
-    hops[0].append(pass_on(0, chunks - 1))
-    for c in range(chunks):
-        for copy in hops[0][c]:
-            copy.wait_recv()
-        hops[1].append(pass_on(1, c))
+        if p >= 1:
+            gathered(p - 1)
+        if p >= 2:
+            forward(p - 2)
+        rel_some(p)
+    gathered(chunks - 1)
+    forward(chunks - 2)
+    forward(chunks - 1)
     loads[5].wait()
     for c in range(chunks):
         for copy in hops[1][c]:
@@ -381,8 +403,8 @@
             pltpu.VMEM((chunks, 8, ROWS), F32),
             pltpu.VMEM((3, chunks, 8, ROWS), F32),
             dma((6,)),
-            dma((3, chunks)),
-            dma((3, chunks)),
+            dma((3, 2 * chunks)),
+            dma((3, 2 * chunks)),
             dma((2, 2, chunks)),
             dma((2, 2, chunks)),
             dma((3, chunks)),

time: 101 us -> 98.2 us (0.972)
  Pallas kernels: 99 us -> 96.1 us
    pallas_call x1, Pallas kernels: 99 us -> 96.1 us  [shards(): pl.pallas_call(functools.partial(kernel, n_seq, n_tp), out_shape=jax.Shap...]
where the time goes in v2:
time: 98.2 us; the launch traced here: 98 us
  Pallas kernels  96.1 us (98%)
  local copies, waits for them, and re-layouts  1.87 us (2%)
    pallas_call x1, Pallas kernels, shards(): pl.pallas_call(functools.partial(kernel, n_seq, n_tp), out_shape=jax.Shap...  96.1 us

profile of v2, /device:TPU:0, one launch (start us, length us, event | category | flops | bytes accessed | tf_op | source)
XLA Modules:
  0.0 98.0 jit_solution(12670710306130204058)
XLA Ops:
  0.0 96.1 %layer.1 = bf16[512,512]{1,0:T(8,128)(2,1)} custom-call(bf16[512,512]{1,0:T(8,128)(2,1)} %hidden.1, bf16[2048,512]{1,0:T(8,128)(2,1)} %wq_hbm.1, bf16[2048,512]{1,0:T(8,128)(2,1)} %wk_hbm.1, bf16[2048,512]{1,0:T(8,128)(2,1)} %wv_hbm.1, bf16[2048,512]{1,0:T(8,128)(2,1)} %wpos_hbm.1, bf16[512,2048]{1,0:T(8,128)(2,1)} %wout_hbm.1, ...), custom_call_target="tpu_custom_call" | custom-call | tf_op jit(solution)/shard_map/layer/pallas_call | solution.py:382
  96.1 1.9 %copy.14 = bf16[512,512]{1,0:T(8,128)(2,1)} copy(bf16[512,512]{1,0:T(8,128)(2,1)} %layer.1) | data formatting | bytes 1048576
